TPU v7x, 256 devices: a whole 4x4x8 slice. The times are simulated.
256 devices in a mesh: tm: 128 (over x, y_hi, z, core), chan: 2 (over y_lo).
Axes of the slice: x: 4, y: 4 (y_hi: 2, y_lo: 2; y = y_hi * 2 + y_lo), z: 8, core: 2. Of those that a mesh axis runs over, the one named last changes fastest.
Arguments:
- random_forcing: bfloat16 [49152, 4096], P('tm', 'chan'), may hold values from -6 to 6
- eigen_root_table: float32 [768, 4096], P(None, 'chan'), may hold values from 0.1 to 2
- lane_fading_speed: float32 [4096], P('chan'), may hold values from 4.0690104e-08 to 0.025, as said below
- sudden_shrink: float32 [49152], P('tm'), may hold values from 0.125 to 1, as said below
Outputs:
- sample: float32 [49152, 4096], P('tm', 'chan')
Inputs may be any that keep to these rules, and one draw needn't show every extreme that they name: `lane_fading_speed`: every channel's rate is positive. `sudden_shrink`: every entry lies in (0, 1], and the product of all entries is at most 0.52.
All inputs are finite; a program needn't handle non-finite values.
Results may differ from a plain program's by a relative error of at most 0.0003.
Values may be sent and summed in bfloat16 or wider, within the bound.
A program may use at most 192 MiB of HBM per device.

v0:
```python
import jax
import jax.numpy as jnp
from jax import lax
from jax.sharding import Mesh
from jax.sharding import PartitionSpec as P

TM = ("tm_0", "tm_1", "tm_2", "tm_3")


def from_behind(value, axis, steps):
    count = lax.axis_size(axis)
    pairs = [(source, (source + steps) % count) for source in range(count)]
    return lax.ppermute(value, axis, pairs)


def filled_with(array, identity):
    return jax.tree.map(
        lambda a, e: jnp.broadcast_to(jnp.asarray(e, a.dtype), a.shape), array, identity
    )


def collected_together(array, axis):
    leaves = jax.tree.leaves(array)
    order = sorted(range(len(leaves)), key=lambda k: -leaves[k].size)
    width = (1, *leaves[order[0]].shape)[-1]
    lines = [
        jnp.pad(leaves[k].reshape(-1), (0, -leaves[k].size % width)).reshape(-1, width)
        for k in order
    ]
    both, at, found = (lax.all_gather(jnp.concatenate(lines), axis), 0, {})
    for k, line in zip(order, lines):
        slab = both[:, at : at + len(line)].reshape(len(both), -1)
        found[k] = slab[:, : leaves[k].size].reshape(-1, *leaves[k].shape)
        at += len(line)
    numbers = iter(range(len(leaves)))
    return jax.tree.map(lambda _: found[next(numbers)], array)


def carried_in(array, axes, combine, identity):
    before = start = filled_with(array, identity)
    so_far = array
    for axis in reversed(axes):
        peers, position = (lax.axis_size(axis), lax.axis_index(axis))
        pieces = collected_together(so_far, axis)
        inside, so_far = (start, start)
        for k in range(peers):
            passed = k < position
            so_far = combine(so_far, jax.tree.map(lambda part: part[k], pieces))
            inside = jax.tree.map(lambda new, old: jnp.where(passed, new, old), so_far, inside)
        before = combine(inside, before)
    return before


def from_root(array, axes, root):
    array = jnp.where(lax.axis_index(axes) == root, array, jnp.zeros_like(array))
    for axis in axes:
        array = lax.psum(array, axis)
    return array


def combine(former, latter):
    return (former[0] + latter[0], jnp.exp(latter[0]) * former[1] + latter[1])


def tables(length):
    indices = jnp.arange(2 * length, dtype=jnp.int32)
    product = indices[:, None] * indices[None, :] % (2 * length)
    angles = product.astype(jnp.float32) * (jnp.pi / length)
    cosine = jnp.cos(angles)
    sine_table = jnp.sin(angles)
    forward = jnp.concatenate([cosine[:, :length], -sine_table[:, :length]], axis=0)
    inverse = jnp.concatenate([cosine, -sine_table], axis=1) / (2.0 * length)
    return (forward, inverse)


def spectra(segment, forward, spectrum, length):
    values = jnp.dot(
        forward,
        segment.astype(jnp.float32),
        precision=lax.Precision.HIGHEST,
        preferred_element_type=jnp.float32,
    )
    return jnp.concatenate(
        [spectrum * values[: 2 * length], spectrum * values[2 * length :]], axis=0
    )


def invert(scaled, inverse, first, count):
    return jnp.dot(
        inverse[first : first + count],
        scaled,
        precision=lax.Precision.HIGHEST,
        preferred_element_type=jnp.float32,
    )


def shards(random_forcing, eigen_root_table, lane_fading_speed, sudden_shrink):
    length = random_forcing.shape[0]
    width = random_forcing.shape[1]
    forward, inverse = tables(length)
    earlier_noise = from_behind(random_forcing, TM, 1)
    stacked = jnp.concatenate([random_forcing, earlier_noise], axis=1)
    doubled = jnp.concatenate([eigen_root_table, eigen_root_table], axis=1)
    scaled = spectra(stacked, forward, doubled, length)
    own_part = invert(scaled[:, :width], inverse, 0, length)
    earlier_part = invert(scaled[:, width:], inverse, length, length)
    noise_sequence = own_part + earlier_part
    tick_log_growth = jnp.log(sudden_shrink)[:, None] - lane_fading_speed[None, :]
    power_entries = (sudden_shrink * sudden_shrink)[:, None]
    weights = jnp.sqrt(
        1.0 - power_entries + power_entries * (-jnp.expm1(-2.0 * lane_fading_speed))[None, :]
    )
    rows = jnp.arange(length, dtype=jnp.int32)
    lower = (rows[:, None] >= rows[None, :]).astype(jnp.float32)
    logs = jnp.dot(
        lower, tick_log_growth, precision=lax.Precision.HIGHEST, preferred_element_type=jnp.float32
    )
    rescaled = jnp.exp(-logs) * (weights * noise_sequence)
    states = jnp.exp(logs) * jnp.dot(
        lower, rescaled, precision=lax.Precision.HIGHEST, preferred_element_type=jnp.float32
    )
    own_total = (logs[-1], states[-1])
    zeroes = jnp.zeros_like(own_total[0])
    preceding_input = carried_in(own_total, TM, combine, (zeroes, zeroes))
    through = combine(preceding_input, own_total)
    entire = (
        from_root(through[0], TM, lax.axis_size(TM) - 1),
        from_root(through[1], TM, lax.axis_size(TM) - 1),
    )
    opening = entire[1] / -jnp.expm1(entire[0])
    incoming = jnp.exp(preceding_input[0]) * opening + preceding_input[1]
    return states + jnp.exp(logs) * incoming[None, :]


def solution(mesh):
    torus = Mesh(
        mesh.devices.reshape(4, 2, 8, 2, mesh.shape["chan"]),
        ("tm_0", "tm_1", "tm_2", "tm_3", "chan"),
    )
    return jax.shard_map(
        shards,
        mesh=torus,
        in_specs=(P(TM, "chan"), P(None, "chan"), P("chan"), P(TM)),
        out_specs=P(TM, "chan"),
        check_vma=False,
    )
```

profile of v0, /device:TPU:1, one launch (start us, length us, event | category | flops | bytes accessed | tf_op | source)
XLA Modules:
  0.0 237.6 jit_solution(13609140888398446958)
XLA Ops:
  0.0 3.0 %collective-permute-start = (bf16[384,2048]{1,0:T(8,128)(2,1)}, bf16[384,2048]{1,0:T(8,128)(2,1)}, u32[]{:S(2)}, u32[]{:S(2)}) collective-permute-start(bf16[384,2048]{1,0:T(8,128)(2,1)} %param.4), channel_id=1, source_target_pairs={{0,2},{2,4},{4,6},{6,8},{8,10},{10,12},{12,14},{14,16},{16,18},{18... | collective-permute-start | bytes 4718600 | tf_op jit(solution)/shard_map/ppermute | solution.py:13
  3.0 10.5 %fusion.32 = (f32[768,768]{1,0:T(8,128)S(1)}, f32[768,768]{1,0:T(8,128)}) fusion(), kind=kLoop, calls=%fused_computation.39 | loop fusion | flops 5898240 | bytes 4718592 | tf_op jit(solution)/shard_map/cos | solution.py:69
  13.5 0.1 slice.241
  13.6 0.0 copy-done.12
  13.6 0.6 broadcast_subtract_fusion
  14.2 0.0 copy-done.11
  14.2 2.9 %fusion.18 = f32[384,2048]{1,0:T(8,128)S(1)} fusion(f32[2048]{0:T(1024)S(1)} %copy-done.11, f32[384]{0:T(512)S(1)} %get-tuple-element.39), kind=kOutput, calls=%fused_computation.25 | convolution fusion | flops 3624812544 | bytes 3155456 | tf_op jit(solution)/shard_map/dot_general | solution.py:115
  17.1 0.0 copy-start.3
  17.1 1.7 copy-done.3
  18.8 9.1 %fusion.31 = f32[768,768]{1,0:T(8,128)S(1)} fusion(), kind=kLoop, calls=%fused_computation.38 | loop fusion | flops 5308416 | bytes 2359296 | tf_op jit(solution)/shard_map/sin | solution.py:70
  27.9 0.0 slice-start
  27.9 0.1 slice_negate_fusion
  28.0 0.0 slice-start.1
  28.0 3.4 %constant_dynamic-update-slice_fusion.1 = f32[768,4096]{1,0:T(8,128)S(1)} fusion(f32[768,2048]{1,0:T(8,128)} %param.5), kind=kLoop, calls=%fused_computation.112 | loop fusion | bytes 12582912
  31.4 0.5 slice-done
  31.9 0.7 slice-done.1
  32.6 0.8 constant_dynamic-update-slice_fusion
  33.4 0.0 copy-start.1
  33.4 0.9 copy-done.7
  34.3 2.8 %maximum_multiply_fusion = f32[768,1536]{1,0:T(8,128)} fusion(f32[768,768]{1,0:T(8,128)S(1)} %copy-done.7, f32[768,768]{1,0:T(8,128)S(1)} %get-tuple-element.40), kind=kLoop, calls=%fused_computation.9 | loop fusion | flops 2359296 | bytes 9437184 | tf_op jit(solution)/shard_map/div | solution.py:72
  37.1 0.0 collective-permute-done
  37.1 2.5 %copy-done.1 = f32[768,4096]{1,0:T(8,128)} copy-done((f32[768,4096]{1,0:T(8,128)}, f32[768,4096]{1,0:T(8,128)S(1)}, u32[]{:S(2)}) %copy-start.1) | copy-done | bytes 12582936
  39.6 0.0 copy-done.8
  39.6 23.3 %fusion.5 = f32[1536,4096]{1,0:T(8,128)} fusion(bf16[384,2048]{1,0:T(8,128)(2,1)} %collective-permute-done, bf16[384,2048]{1,0:T(8,128)(2,1)S(1)} %copy-done.8, f32[768,384]{1,0:T(8,128)S(1)} %slice_negate_fusion, f32[768,384]{1,0:T(8,128)S(1)} %slice.241), kind=kOutput, calls=%fused_computation.11 | convolution fusion | flops 28997910528 | bytes 30670848 | tf_op jit(solution)/shard_map/dot_general | solution.py:77
  62.9 18.3 %slice_multiply_fusion = (f32[768,4096]{1,0:T(8,128)S(1)}, f32[768,4096]{1,0:T(8,128)}) fusion(f32[768,4096]{1,0:T(8,128)} %copy-done.1, f32[1536,4096]{1,0:T(8,128)} %fusion.5), kind=kLoop, calls=%fused_computation.7 | loop fusion | flops 6291456 | bytes 62914560 | tf_op jit(solution)/shard_map/mul | solution.py:84
  81.3 19.2 %fusion.3 = f32[384,2048]{1,0:T(8,128)} fusion(f32[768,4096]{1,0:T(8,128)S(1)} %get-tuple-element.28, f32[768,4096]{1,0:T(8,128)} %get-tuple-element.29, f32[768,1536]{1,0:T(8,128)} %maximum_multiply_fusion), kind=kOutput, calls=%fused_computation.5 | convolution fusion | flops 14498660352 | bytes 30670848 | tf_op jit(solution)/shard_map/dot_general | solution.py:89
  100.4 0.0 copy-done
  100.5 0.0 copy-done.2
  100.5 0.0 copy-start.9
  100.5 0.0 copy-start.10
  100.5 17.2 %fusion.1 = f32[384,2048]{1,0:T(8,128)} fusion(f32[768,4096]{1,0:T(8,128)S(1)} %copy-done, f32[768,4096]{1,0:T(8,128)S(1)} %get-tuple-element.28, f32[768,1536]{1,0:T(8,128)S(1)} %copy-done.2), kind=kOutput, calls=%fused_computation.3 | convolution fusion | flops 14498660352 | bytes 30670848 | tf_op jit(solution)/shard_map/dot_general | solution.py:89
  117.7 0.0 copy-done.4
  117.7 0.0 copy-start.5
  117.7 6.5 %exponential_multiply_fusion = f32[384,2048]{1,0:T(8,128)S(1)} fusion(f32[384,2048]{1,0:T(8,128)S(1)} %copy-done.4, f32[384,2048]{1,0:T(8,128)} %fusion.1, f32[384,2048]{1,0:T(8,128)} %fusion.3, f32[2048]{0:T(1024)S(1)} %exponential-minus-one_negate_fusion, f32[384]{0:T(512)S(1)} %copy-done.10, f32[384]{0:T(512)S(1)} %copy-done.9), kind=kOutput, calls=%fused_computation.27 | convolution fusion | flops 3629531136 | bytes 12594176 | tf_op jit(solution)/shard_map/dot_general | solution.py:119
  124.2 1.6 copy-done.6
  125.9 1.8 all-gather.4
  127.8 21.2 %all-gather.5 = f32[8,2,2048]{2,1,0:T(2,128)S(1)} all-gather(f32[1,2,2048]{2,1,0:T(2,128)S(1)} %maximum_bitcast_fusion.1), channel_id=3, replica_groups=mesh['tm_0'=4,'tm_1'=2,'tm_2'=8,'tm_3'=2,'chan'=2] {'tm_2'}, dimensions={0}, use_global_device_ids=true | all-gather | bytes 147456 | tf_op jit(solution)/shard_map/all_gather | solution.py:30
  149.0 0.1 fusion.46
  149.1 0.1 broadcast_select_fusion.1
  149.3 4.8 %all-gather.6 = f32[2,2,2048]{2,1,0:T(2,128)S(1)} all-gather(f32[1,2,2048]{2,1,0:T(2,128)S(1)} %maximum_bitcast_fusion.2), channel_id=4, replica_groups=mesh['tm_0'=4,'tm_1'=2,'tm_2'=8,'tm_3'=2,'chan'=2] {'tm_1'}, dimensions={0}, use_global_device_ids=true | all-gather | bytes 49152 | tf_op jit(solution)/shard_map/all_gather | solution.py:30
  154.1 9.3 %all-gather.7 = f32[4,2,2048]{2,1,0:T(2,128)S(1)} all-gather(f32[1,2,2048]{2,1,0:T(2,128)S(1)} %maximum_bitcast_fusion.3), channel_id=5, replica_groups=mesh['tm_0'=4,'tm_1'=2,'tm_2'=8,'tm_3'=2,'chan'=2] {'tm_0'}, dimensions={0}, use_global_device_ids=true | all-gather | bytes 81920 | tf_op jit(solution)/shard_map/all_gather | solution.py:30
  163.4 0.1 fusion.40
  163.5 0.1 fusion.41
  163.7 12.8 %all-reduce.1 = (f32[2048]{0:T(1024)S(1)}, f32[2048]{0:T(1024)S(1)}) all-reduce(f32[2048]{0:T(1024)S(1)} %get-tuple-element.16, f32[2048]{0:T(1024)S(1)} %get-tuple-element.36), channel_id=1, replica_groups=mesh['tm_0'=4,'tm_1'=2,'tm_2'=8,'tm_3'=2,'chan'=2] {'tm_0'}, use_global_device_ids=true, to_apply=%region_0.1 | all-reduce | flops 4096 | bytes 32768 | tf_op jit(solution)/shard_map/psum | solution.py:57
  176.5 9.2 %all-reduce.3 = (f32[2048]{0:T(1024)S(1)}, f32[2048]{0:T(1024)S(1)}) all-reduce(f32[2048]{0:T(1024)S(1)} %get-tuple-element.7, f32[2048]{0:T(1024)S(1)} %get-tuple-element.8), channel_id=1, replica_groups=mesh['tm_0'=4,'tm_1'=2,'tm_2'=8,'tm_3'=2,'chan'=2] {'tm_1'}, use_global_device_ids=true, to_apply=%region_1.2 | all-reduce | flops 4096 | bytes 32768 | tf_op jit(solution)/shard_map/psum | solution.py:57
  185.7 20.9 %all-reduce = (f32[2048]{0:T(1024)S(1)}, f32[2048]{0:T(1024)S(1)}) all-reduce(f32[2048]{0:T(1024)S(1)} %get-tuple-element.11, f32[2048]{0:T(1024)S(1)} %get-tuple-element.12), channel_id=1, replica_groups=mesh['tm_0'=4,'tm_1'=2,'tm_2'=8,'tm_3'=2,'chan'=2] {'tm_2'}, use_global_device_ids=true, to_apply=%region_2.3 | all-reduce | flops 4096 | bytes 32768 | tf_op jit(solution)/shard_map/psum | solution.py:57
  206.7 26.6 %all-reduce.2 = (f32[2048]{0:T(1024)S(1)}, f32[2048]{0:T(1024)S(1)}) all-reduce(f32[2048]{0:T(1024)S(1)} %get-tuple-element.5, f32[2048]{0:T(1024)S(1)} %get-tuple-element.6), channel_id=1, replica_groups=mesh['tm_0'=4,'tm_1'=2,'tm_2'=8,'tm_3'=2,'chan'=2] {'tm_3'}, use_global_device_ids=true, to_apply=%region_3.4 | all-reduce | flops 4096 | bytes 32768 | tf_op jit(solution)/shard_map/psum | solution.py:57
  233.3 4.3 %multiply_add_fusion = f32[384,2048]{1,0:T(8,128)} fusion(f32[384,2048]{1,0:T(8,128)} %copy-done.6, f32[384,2048]{1,0:T(8,128)S(1)} %copy-done.5, f32[2048]{0:T(1024)S(1)} %multiply_add_fusion.1), kind=kLoop, calls=%fused_computation.15 | loop fusion | flops 1572864 | bytes 9445376 | tf_op jit(solution)/shard_map/add | solution.py:132
  (26 shorter events, 0.3 us)
Async XLA Ops:
  0.0 13.6 %copy-start.12 = (f32[384]{0:T(512)S(1)}, f32[384]{0:T(512)}, u32[]{:S(2)}) copy-start(f32[384]{0:T(512)} %param.7) | copy-start | bytes 4612
  0.0 14.2 %copy-start.11 = (f32[2048]{0:T(1024)S(1)}, f32[2048]{0:T(1024)}, u32[]{:S(2)}) copy-start(f32[2048]{0:T(1024)} %param.6) | copy-start | bytes 24580
  0.0 37.1 %collective-permute-start = (bf16[384,2048]{1,0:T(8,128)(2,1)}, bf16[384,2048]{1,0:T(8,128)(2,1)}, u32[]{:S(2)}, u32[]{:S(2)}) collective-permute-start(bf16[384,2048]{1,0:T(8,128)(2,1)} %param.4), channel_id=1, source_target_pairs={{0,2},{2,4},{4,6},{6,8},{8,10},{10,12},{12,14},{14,16},{16,18},{18... | collective-permute-start | bytes 4718600 | tf_op jit(solution)/shard_map/ppermute | solution.py:13
  17.1 1.7 copy-start.3
  27.9 4.0 %slice-start = ((s8[6291456]{0:T(1024)(128)(4,1)}), s8[4194304]{0:T(1024)(128)(4,1)S(1)}, s32[]{:S(2)}) async-start(s8[6291456]{0:T(1024)(128)(4,1)} %bitcast.30), calls=%async_computation | async-start | bytes 8388608
  28.0 4.6 %slice-start.1 = ((s8[6291456]{0:T(1024)(128)(4,1)}), s8[2097152]{0:T(1024)(128)(4,1)S(1)}, s32[]{:S(2)}) async-start(s8[6291456]{0:T(1024)(128)(4,1)} %bitcast.30), calls=%async_computation.1 | async-start | bytes 4194304
  32.6 1.7 copy-start.7
  33.4 6.2 %copy-start.1 = (f32[768,4096]{1,0:T(8,128)}, f32[768,4096]{1,0:T(8,128)S(1)}, u32[]{:S(2)}) copy-start(f32[768,4096]{1,0:T(8,128)S(1)} %constant_dynamic-update-slice_fusion) | copy-start | bytes 37748740
  34.3 5.3 %copy-start.8 = (bf16[384,2048]{1,0:T(8,128)(2,1)S(1)}, bf16[384,2048]{1,0:T(8,128)(2,1)}, u32[]{:S(2)}) copy-start(bf16[384,2048]{1,0:T(8,128)(2,1)} %param.4) | copy-start | bytes 4718596
  81.3 19.2 %copy-start = (f32[768,4096]{1,0:T(8,128)S(1)}, f32[768,4096]{1,0:T(8,128)}, u32[]{:S(2)}) copy-start(f32[768,4096]{1,0:T(8,128)} %get-tuple-element.29) | copy-start | bytes 37748740
  81.3 19.2 %copy-start.2 = (f32[768,1536]{1,0:T(8,128)S(1)}, f32[768,1536]{1,0:T(8,128)}, u32[]{:S(2)}) copy-start(f32[768,1536]{1,0:T(8,128)} %maximum_multiply_fusion) | copy-start | bytes 14155780
  100.5 17.2 %copy-start.4 = (f32[384,2048]{1,0:T(8,128)S(1)}, f32[384,2048]{1,0:T(8,128)}, u32[]{:S(2)}) copy-start(f32[384,2048]{1,0:T(8,128)} %copy-done.3) | copy-start | bytes 9437188
  100.5 17.2 %copy-start.9 = (f32[384]{0:T(512)S(1)}, f32[384]{0:T(512)}, u32[]{:S(2)}) copy-start(f32[384]{0:T(512)} %get-tuple-element.37) | copy-start | bytes 4612
  100.5 17.2 %copy-start.10 = (f32[384]{0:T(512)S(1)}, f32[384]{0:T(512)}, u32[]{:S(2)}) copy-start(f32[384]{0:T(512)} %get-tuple-element.38) | copy-start | bytes 4612
  117.7 115.6 %copy-start.5 = (f32[384,2048]{1,0:T(8,128)S(1)}, f32[384,2048]{1,0:T(8,128)}, u32[]{:S(2)}) copy-start(f32[384,2048]{1,0:T(8,128)} %copy-done.3) | copy-start | bytes 9437188
  124.2 1.7 copy-start.6
where the time goes:
time: 238 us
  blocking collectives  107 us (45%)
  matrix products  69.1 us (29%)
  other arithmetic  46.3 us (19%)
  local copies, waits for them, and re-layouts  12.2 us (5%)
  starting transfers between devices  3.02 us (1%)
    psum x4, blocking collectives, from_root(): array = lax.psum(array, axis)  69.6 us
    all_gather x4, blocking collectives, collected_together(): both, at, found = (lax.all_gather(jnp.concatenate(lines), axis), 0, {})  37.1 us
    dot_general x2, matrix products, invert(): jnp.dot(inverse[first:first + count], scaled, precision=lax.Precision.HIG...  36.4 us
    dot_general x1, matrix products, spectra(): jnp.dot(forward, segment.astype(jnp.float32), precision=lax.Precision.HIG...  23.3 us
    mul x1, other arithmetic, spectra(): spectrum * values[2 * length:]  18.3 us
    unnamed x31, local copies, waits for them, and re-layouts  11.3 us
    cos x1, other arithmetic, tables(): cosine = jnp.cos(angles)  10.5 us
    sin x1, other arithmetic, tables(): sine_table = jnp.sin(angles)  9.06 us
  transfers between devices with their start and end apart: 1, of which 0 were waited for; matrix products, arithmetic and copies ran while one was open for 13% of the time, Pallas kernels for 0%

commit v1 on v0

--- a/solution.py
+++ b/solution.py
@@ -54,7 +54,7 @@
 def from_root(array, axes, root):
     array = jnp.where(lax.axis_index(axes) == root, array, jnp.zeros_like(array))
     for axis in axes:
-        array = lax.psum(array, axis)
+        array = jnp.sum(lax.all_gather(array, axis), axis=0)
     return array
 
 

time: 238 us -> 265 us (1.11)
  blocking collectives: 107 us -> 135 us
    all_gather x0 -> x8, blocking collectives: none -> 98.4 us  [from_root(): array = jnp.sum(lax.all_gather(array, axis), axis=0)]
    psum x4 -> x0, blocking collectives: 69.6 us -> none  [from_root(): array = lax.psum(array, axis)]
  transfers between devices with their start and end apart: 1 -> 1, of which waited for: 0 -> 0; matrix products, arithmetic and copies ran while one was open for 13% -> 11% of each run, Pallas kernels for 0% -> 0%
where the time goes in v1:
time: 265 us
  blocking collectives  135 us (51%)
  matrix products  69.1 us (26%)
  other arithmetic  46.6 us (18%)
  local copies, waits for them, and re-layouts  10.6 us (4%)
  starting transfers between devices  3.02 us (1%)
    all_gather x8, blocking collectives, from_root(): array = jnp.sum(lax.all_gather(array, axis), axis=0)  98.4 us
    all_gather x4, blocking collectives, collected_together(): both, at, found = (lax.all_gather(jnp.concatenate(lines), axis), 0, {})  37.1 us
    dot_general x2, matrix products, invert(): jnp.dot(inverse[first:first + count], scaled, precision=lax.Precision.HIG...  36.4 us
    dot_general x1, matrix products, spectra(): jnp.dot(forward, segment.astype(jnp.float32), precision=lax.Precision.HIG...  23.3 us
    mul x1, other arithmetic, spectra(): spectrum * values[2 * length:]  18.3 us
    cos x1, other arithmetic, tables(): cosine = jnp.cos(angles)  10.5 us
    unnamed x31, local copies, waits for them, and re-layouts  9.67 us
    sin x1, other arithmetic, tables(): sine_table = jnp.sin(angles)  9.06 us
  transfers between devices with their start and end apart: 1, of which 0 were waited for; matrix products, arithmetic and copies ran while one was open for 11% of the time, Pallas kernels for 0%

profile of v1, /device:TPU:1, one launch (start us, length us, event | category | flops | bytes accessed | tf_op | source)
XLA Modules:
  0.0 265.2 jit_solution(4006991591550160351)
XLA Ops:
  0.0 3.0 %collective-permute-start = (bf16[384,2048]{1,0:T(8,128)(2,1)}, bf16[384,2048]{1,0:T(8,128)(2,1)}, u32[]{:S(2)}, u32[]{:S(2)}) collective-permute-start(bf16[384,2048]{1,0:T(8,128)(2,1)} %param.4), channel_id=1, source_target_pairs={{0,2},{2,4},{4,6},{6,8},{8,10},{10,12},{12,14},{14,16},{16,18},{18... | collective-permute-start | bytes 4718600 | tf_op jit(solution)/shard_map/ppermute | solution.py:13
  3.0 10.5 %fusion.32 = (f32[768,768]{1,0:T(8,128)S(1)}, f32[768,768]{1,0:T(8,128)}) fusion(), kind=kLoop, calls=%fused_computation.39 | loop fusion | flops 5898240 | bytes 4718592 | tf_op jit(solution)/shard_map/cos | solution.py:69
  13.5 0.1 slice.241
  13.6 0.0 copy-done.12
  13.6 0.6 broadcast_subtract_fusion
  14.2 0.0 copy-done.11
  14.2 2.9 %fusion.18 = f32[384,2048]{1,0:T(8,128)S(1)} fusion(f32[2048]{0:T(1024)S(1)} %copy-done.11, f32[384]{0:T(512)S(1)} %get-tuple-element.36), kind=kOutput, calls=%fused_computation.25 | convolution fusion | flops 3624812544 | bytes 3155456 | tf_op jit(solution)/shard_map/dot_general | solution.py:115
  17.1 0.0 copy-start.3
  17.1 1.7 copy-done.3
  18.8 9.1 %fusion.31 = f32[768,768]{1,0:T(8,128)S(1)} fusion(), kind=kLoop, calls=%fused_computation.38 | loop fusion | flops 5308416 | bytes 2359296 | tf_op jit(solution)/shard_map/sin | solution.py:70
  27.9 0.0 slice-start
  27.9 0.1 slice_negate_fusion
  28.0 0.0 slice-start.1
  28.0 3.4 %constant_dynamic-update-slice_fusion.1 = f32[768,4096]{1,0:T(8,128)S(1)} fusion(f32[768,2048]{1,0:T(8,128)} %param.5), kind=kLoop, calls=%fused_computation.129 | loop fusion | bytes 12582912
  31.4 0.5 slice-done
  31.9 0.7 slice-done.1
  32.6 0.8 constant_dynamic-update-slice_fusion
  33.4 0.0 copy-start.1
  33.4 0.9 copy-done.7
  34.3 2.8 %maximum_multiply_fusion = f32[768,1536]{1,0:T(8,128)} fusion(f32[768,768]{1,0:T(8,128)S(1)} %copy-done.7, f32[768,768]{1,0:T(8,128)S(1)} %get-tuple-element.37), kind=kLoop, calls=%fused_computation.9 | loop fusion | flops 2359296 | bytes 9437184 | tf_op jit(solution)/shard_map/div | solution.py:72
  37.1 0.0 collective-permute-done
  37.1 2.5 copy-done.1
  39.6 0.0 copy-done.8
  39.6 23.3 %fusion.5 = f32[1536,4096]{1,0:T(8,128)} fusion(bf16[384,2048]{1,0:T(8,128)(2,1)} %collective-permute-done, bf16[384,2048]{1,0:T(8,128)(2,1)S(1)} %copy-done.8, f32[768,384]{1,0:T(8,128)S(1)} %slice_negate_fusion, f32[768,384]{1,0:T(8,128)S(1)} %slice.241), kind=kOutput, calls=%fused_computation.11 | convolution fusion | flops 28997910528 | bytes 30670848 | tf_op jit(solution)/shard_map/dot_general | solution.py:77
  62.9 18.3 %slice_multiply_fusion = (f32[768,4096]{1,0:T(8,128)S(1)}, f32[768,4096]{1,0:T(8,128)}) fusion(f32[768,4096]{1,0:T(8,128)} %copy-done.1, f32[1536,4096]{1,0:T(8,128)} %fusion.5), kind=kLoop, calls=%fused_computation.7 | loop fusion | flops 6291456 | bytes 62914560 | tf_op jit(solution)/shard_map/mul | solution.py:84
  81.2 19.2 %fusion.3 = f32[384,2048]{1,0:T(8,128)} fusion(f32[768,4096]{1,0:T(8,128)S(1)} %get-tuple-element.26, f32[768,4096]{1,0:T(8,128)} %get-tuple-element.27, f32[768,1536]{1,0:T(8,128)} %maximum_multiply_fusion), kind=kOutput, calls=%fused_computation.5 | convolution fusion | flops 14498660352 | bytes 30670848 | tf_op jit(solution)/shard_map/dot_general | solution.py:89
  100.4 0.0 copy-done
  100.5 17.2 %fusion.1 = f32[384,2048]{1,0:T(8,128)} fusion(f32[768,4096]{1,0:T(8,128)S(1)} %copy-done, f32[768,4096]{1,0:T(8,128)S(1)} %get-tuple-element.26, f32[768,1536]{1,0:T(8,128)S(1)} %copy-done.2), kind=kOutput, calls=%fused_computation.3 | convolution fusion | flops 14498660352 | bytes 30670848 | tf_op jit(solution)/shard_map/dot_general | solution.py:89
  117.6 0.0 copy-done.9
  117.6 0.0 copy-start.5
  117.7 6.5 %exponential_multiply_fusion = f32[384,2048]{1,0:T(8,128)S(1)} fusion(f32[384,2048]{1,0:T(8,128)S(1)} %copy-done.4, f32[384,2048]{1,0:T(8,128)} %fusion.1, f32[384,2048]{1,0:T(8,128)} %fusion.3, f32[2048]{0:T(1024)S(1)} %exponential-minus-one_negate_fusion, f32[384]{0:T(512)S(1)} %copy-done.10, f32[384]{0:T(512)S(1)} %copy-done.9), kind=kOutput, calls=%fused_computation.27 | convolution fusion | flops 3629531136 | bytes 12594176 | tf_op jit(solution)/shard_map/dot_general | solution.py:119
  124.2 0.0 copy-start.6
  124.3 1.8 all-gather.10
  126.2 21.2 %all-gather.11 = f32[8,2,2048]{2,1,0:T(2,128)S(1)} all-gather(f32[1,2,2048]{2,1,0:T(2,128)S(1)} %maximum_bitcast_fusion.1), channel_id=3, replica_groups=mesh['tm_0'=4,'tm_1'=2,'tm_2'=8,'tm_3'=2,'chan'=2] {'tm_2'}, dimensions={0}, use_global_device_ids=true | all-gather | bytes 147456 | tf_op jit(solution)/shard_map/all_gather | solution.py:30
  147.4 0.1 bitcast_add_fusion.1
  147.6 4.8 %all-gather.12 = f32[2,2,2048]{2,1,0:T(2,128)S(1)} all-gather(f32[1,2,2048]{2,1,0:T(2,128)S(1)} %maximum_bitcast_fusion.2), channel_id=4, replica_groups=mesh['tm_0'=4,'tm_1'=2,'tm_2'=8,'tm_3'=2,'chan'=2] {'tm_1'}, dimensions={0}, use_global_device_ids=true | all-gather | bytes 49152 | tf_op jit(solution)/shard_map/all_gather | solution.py:30
  152.4 9.3 %all-gather.13 = f32[4,2,2048]{2,1,0:T(2,128)S(1)} all-gather(f32[1,2,2048]{2,1,0:T(2,128)S(1)} %maximum_bitcast_fusion.3), channel_id=5, replica_groups=mesh['tm_0'=4,'tm_1'=2,'tm_2'=8,'tm_3'=2,'chan'=2] {'tm_0'}, dimensions={0}, use_global_device_ids=true | all-gather | bytes 81920 | tf_op jit(solution)/shard_map/all_gather | solution.py:30
  161.7 0.1 fusion.43
  161.8 0.3 fusion.42
  162.1 9.0 %all-gather.14 = f32[4,1,2048]{2,1,0:T(1,128)S(1)} all-gather(f32[1,1,2048]{2,1,0:T(1,128)S(1)} %get-tuple-element.9), channel_id=1, replica_groups=mesh['tm_0'=4,'tm_1'=2,'tm_2'=8,'tm_3'=2,'chan'=2] {'tm_0'}, dimensions={0}, use_global_device_ids=true | all-gather | bytes 40960 | tf_op jit(solution)/shard_map/all_gather | solution.py:57
  171.2 4.7 %all-gather.4 = f32[4096]{0:T(1024)S(1)} all-gather(f32[2048]{0:T(1024)S(1)} %reduce_sum.72), channel_id=6, replica_groups=mesh['tm_0'=4,'tm_1'=2,'tm_2'=8,'tm_3'=2,'chan'=2] {'tm_1'}, dimensions={0}, use_global_device_ids=true | all-gather | bytes 24576 | tf_op jit(solution)/shard_map/all_gather | solution.py:57
  175.9 18.5 %all-gather.5 = f32[16384]{0:T(1024)S(1)} all-gather(f32[2048]{0:T(1024)S(1)} %reduce_sum.73), channel_id=7, replica_groups=mesh['tm_0'=4,'tm_1'=2,'tm_2'=8,'tm_3'=2,'chan'=2] {'tm_2'}, dimensions={0}, use_global_device_ids=true | all-gather | bytes 73728 | tf_op jit(solution)/shard_map/all_gather | solution.py:57
  194.5 21.9 %all-gather.6 = f32[4096]{0:T(1024)S(1)} all-gather(f32[2048]{0:T(1024)S(1)} %reduce_sum.74), channel_id=8, replica_groups=mesh['tm_0'=4,'tm_1'=2,'tm_2'=8,'tm_3'=2,'chan'=2] {'tm_3'}, dimensions={0}, use_global_device_ids=true | all-gather | bytes 24576 | tf_op jit(solution)/shard_map/all_gather | solution.py:57
  216.4 9.0 %all-gather.15 = f32[4,1,2048]{2,1,0:T(1,128)S(1)} all-gather(f32[1,1,2048]{2,1,0:T(1,128)S(1)} %get-tuple-element.5), channel_id=1, replica_groups=mesh['tm_0'=4,'tm_1'=2,'tm_2'=8,'tm_3'=2,'chan'=2] {'tm_0'}, dimensions={0}, use_global_device_ids=true | all-gather | bytes 40960 | tf_op jit(solution)/shard_map/all_gather | solution.py:57
  225.5 4.7 %all-gather.7 = f32[4096]{0:T(1024)S(1)} all-gather(f32[2048]{0:T(1024)S(1)} %reduce_sum.76), channel_id=9, replica_groups=mesh['tm_0'=4,'tm_1'=2,'tm_2'=8,'tm_3'=2,'chan'=2] {'tm_1'}, dimensions={0}, use_global_device_ids=true | all-gather | bytes 24576 | tf_op jit(solution)/shard_map/all_gather | solution.py:57
  230.3 18.2 %all-gather.8 = f32[16384]{0:T(1024)S(1)} all-gather(f32[2048]{0:T(1024)S(1)} %reduce_sum.77), channel_id=10, replica_groups=mesh['tm_0'=4,'tm_1'=2,'tm_2'=8,'tm_3'=2,'chan'=2] {'tm_2'}, dimensions={0}, use_global_device_ids=true | all-gather | bytes 73728 | tf_op jit(solution)/shard_map/all_gather | solution.py:57
  248.5 12.2 %all-gather.9 = f32[4096]{0:T(1024)S(1)} all-gather(f32[2048]{0:T(1024)S(1)} %reduce_sum.78), channel_id=11, replica_groups=mesh['tm_0'=4,'tm_1'=2,'tm_2'=8,'tm_3'=2,'chan'=2] {'tm_3'}, dimensions={0}, use_global_device_ids=true | all-gather | bytes 24576 | tf_op jit(solution)/shard_map/all_gather | solution.py:57
  261.0 4.3 %multiply_add_fusion = f32[384,2048]{1,0:T(8,128)} fusion(f32[384,2048]{1,0:T(8,128)} %copy-done.6, f32[384,2048]{1,0:T(8,128)S(1)} %copy-done.5, f32[2048]{0:T(1024)S(1)} %add_add_fusion), kind=kLoop, calls=%fused_computation.15 | loop fusion | flops 1572864 | bytes 9445376 | tf_op jit(solution)/shard_map/add | solution.py:132
  (43 shorter events, 0.7 us)
Async XLA Ops:
  0.0 13.6 %copy-start.12 = (f32[384]{0:T(512)S(1)}, f32[384]{0:T(512)}, u32[]{:S(2)}) copy-start(f32[384]{0:T(512)} %param.7) | copy-start | bytes 4612
  0.0 14.2 %copy-start.11 = (f32[2048]{0:T(1024)S(1)}, f32[2048]{0:T(1024)}, u32[]{:S(2)}) copy-start(f32[2048]{0:T(1024)} %param.6) | copy-start | bytes 24580
  0.0 37.1 %collective-permute-start = (bf16[384,2048]{1,0:T(8,128)(2,1)}, bf16[384,2048]{1,0:T(8,128)(2,1)}, u32[]{:S(2)}, u32[]{:S(2)}) collective-permute-start(bf16[384,2048]{1,0:T(8,128)(2,1)} %param.4), channel_id=1, source_target_pairs={{0,2},{2,4},{4,6},{6,8},{8,10},{10,12},{12,14},{14,16},{16,18},{18... | collective-permute-start | bytes 4718600 | tf_op jit(solution)/shard_map/ppermute | solution.py:13
  17.1 1.7 copy-start.3
  27.9 4.0 %slice-start = ((s8[6291456]{0:T(1024)(128)(4,1)}), s8[4194304]{0:T(1024)(128)(4,1)S(1)}, s32[]{:S(2)}) async-start(s8[6291456]{0:T(1024)(128)(4,1)} %bitcast.86), calls=%async_computation | async-start | bytes 8388608
  28.0 4.6 %slice-start.1 = ((s8[6291456]{0:T(1024)(128)(4,1)}), s8[2097152]{0:T(1024)(128)(4,1)S(1)}, s32[]{:S(2)}) async-start(s8[6291456]{0:T(1024)(128)(4,1)} %bitcast.86), calls=%async_computation.1 | async-start | bytes 4194304
  32.6 1.7 copy-start.7
  33.4 6.2 %copy-start.1 = (f32[768,4096]{1,0:T(8,128)}, f32[768,4096]{1,0:T(8,128)S(1)}, u32[]{:S(2)}) copy-start(f32[768,4096]{1,0:T(8,128)S(1)} %constant_dynamic-update-slice_fusion) | copy-start | bytes 37748740
  34.3 5.3 %copy-start.8 = (bf16[384,2048]{1,0:T(8,128)(2,1)S(1)}, bf16[384,2048]{1,0:T(8,128)(2,1)}, u32[]{:S(2)}) copy-start(bf16[384,2048]{1,0:T(8,128)(2,1)} %param.4) | copy-start | bytes 4718596
  81.2 19.2 %copy-start = (f32[768,4096]{1,0:T(8,128)S(1)}, f32[768,4096]{1,0:T(8,128)}, u32[]{:S(2)}) copy-start(f32[768,4096]{1,0:T(8,128)} %get-tuple-element.27) | copy-start | bytes 37748740
  81.2 19.2 %copy-start.2 = (f32[768,1536]{1,0:T(8,128)S(1)}, f32[768,1536]{1,0:T(8,128)}, u32[]{:S(2)}) copy-start(f32[768,1536]{1,0:T(8,128)} %maximum_multiply_fusion) | copy-start | bytes 14155780
  100.4 17.2 %copy-start.4 = (f32[384,2048]{1,0:T(8,128)S(1)}, f32[384,2048]{1,0:T(8,128)}, u32[]{:S(2)}) copy-start(f32[384,2048]{1,0:T(8,128)} %copy-done.3) | copy-start | bytes 9437188
  100.4 17.2 %copy-start.9 = (f32[384]{0:T(512)S(1)}, f32[384]{0:T(512)}, u32[]{:S(2)}) copy-start(f32[384]{0:T(512)} %get-tuple-element.34) | copy-start | bytes 4612
  100.4 17.2 %copy-start.10 = (f32[384]{0:T(512)S(1)}, f32[384]{0:T(512)}, u32[]{:S(2)}) copy-start(f32[384]{0:T(512)} %get-tuple-element.35) | copy-start | bytes 4612
  117.6 143.3 %copy-start.5 = (f32[384,2048]{1,0:T(8,128)S(1)}, f32[384,2048]{1,0:T(8,128)}, u32[]{:S(2)}) copy-start(f32[384,2048]{1,0:T(8,128)} %copy-done.3) | copy-start | bytes 9437188
  124.2 37.9 %copy-start.6 = (f32[384,2048]{1,0:T(8,128)}, f32[384,2048]{1,0:T(8,128)S(1)}, u32[]{:S(2)}) copy-start(f32[384,2048]{1,0:T(8,128)S(1)} %exponential_multiply_fusion) | copy-start | bytes 9437188
